TPU v7x, 32 devices: a whole 2x2x4 slice. The times are simulated.
32 devices in a mesh: groups: 2 (over x), gx: 8 (over z, y), gy: 2 (over core).
Axes of the slice: x: 2, y: 2, z: 4, core: 2. Of those that a mesh axis runs over, the one named last changes fastest.
Arguments:
- source: float32 [2, 3, 2, 32, 64, 256], P('groups', None, None, 'gx', 'gy'), parts along dimension 0, may hold values from -12 to 12
- permittivity: float32 [6, 32, 64, 256], P('groups', 'gx', 'gy'), parts along dimension 0, may hold values from 1 to 12
- frequency: float32 [1], replicated, may hold values from 0.25 to 0.6
Outputs:
- solution: float32 [2, 3, 2, 32, 64, 256], P('groups', None, None, 'gx', 'gy'), parts along dimension 0
- residual: float32 [2, 3, 2, 32, 64, 256], P('groups', None, None, 'gx', 'gy'), parts along dimension 0
There are 2 independent parts, one for each index of `groups`. A program takes and returns all parts, laid end to end along the dimension named above; an argument that names none is the same for every part. Nothing has to cross between parts.
All inputs are finite; a program needn't handle non-finite values.
Results may differ from a plain program's by a relative error of at most 0.0003.
Values sent between devices are 32-bit elements; how exact they have to be, the bound alone decides.
A program may use at most 64 MiB of HBM per device.

v0:
```python
import jax
import jax.numpy as jnp
from jax import lax
from jax.sharding import PartitionSpec as P

NZ = 256
PML = 8
ITERS = 3
pml_strength = 2.0


def shifted(array, axis, by):
    devices = lax.axis_size(axis)
    pairs = [(i, i + by) for i in range(devices) if 0 <= i + by < devices]
    return lax.ppermute(array, axis, pairs)


def stretch(points, length, frequency):
    inside = jnp.maximum(jnp.maximum(PML - points, points - (length - PML)), 0.0) / PML
    damping = pml_strength * inside**3 / frequency[:, None]
    factor = 1.0 / (1.0 + damping * damping)
    return jnp.stack([factor, -damping * factor], axis=1)


def orient(coefficient, dimension):
    target = [coefficient.shape[0], 2, 1, 1, 1]
    target[dimension] = coefficient.shape[2]
    return coefficient.reshape(target)


def times_coef(values, coefficient):
    real_part = values[:, 0] * coefficient[:, 0] - values[:, 1] * coefficient[:, 1]
    imag_part = values[:, 0] * coefficient[:, 1] + values[:, 1] * coefficient[:, 0]
    return jnp.stack([real_part, imag_part], axis=1)


def curl_forward(extended, front_x, front_y, front_z):
    centre = extended[:, :, :, :-1, :-1]

    def step_x(component):
        return extended[:, component, :, 1:, :-1] - centre[:, component]

    def step_y(component):
        return extended[:, component, :, :-1, 1:] - centre[:, component]

    def step_z(component):
        cells = centre[:, component]
        above = jnp.concatenate([cells[..., 1:], jnp.zeros_like(cells[..., :1])], axis=-1)
        return above - cells

    curl_x = times_coef(step_y(2), front_y) - times_coef(step_z(1), front_z)
    curl_y = times_coef(step_z(0), front_z) - times_coef(step_x(2), front_x)
    curl_z = times_coef(step_x(1), front_x) - times_coef(step_y(0), front_y)
    return jnp.stack([curl_x, curl_y, curl_z], axis=1)


def curl_backward(padded, back_x, back_y, back_z):
    centre = padded[:, :, :, 1:, 1:]

    def step_x(component):
        return centre[:, component] - padded[:, component, :, :-1, 1:]

    def step_y(component):
        return centre[:, component] - padded[:, component, :, 1:, :-1]

    def step_z(component):
        cells = centre[:, component]
        below = jnp.concatenate([jnp.zeros_like(cells[..., :1]), cells[..., :-1]], axis=-1)
        return cells - below

    out_x = times_coef(step_y(2), back_y) - times_coef(step_z(1), back_z)
    out_y = times_coef(step_z(0), back_z) - times_coef(step_x(2), back_x)
    out_z = times_coef(step_x(1), back_x) - times_coef(step_y(0), back_y)
    return jnp.stack([out_x, out_y, out_z], axis=1)


def scaled(values, number):
    real_scale = number[0].reshape(-1, 1, 1, 1, 1)
    imag_scale = number[1].reshape(-1, 1, 1, 1, 1)
    real_part = values[:, :, 0] * real_scale - values[:, :, 1] * imag_scale
    imag_part = values[:, :, 0] * imag_scale + values[:, :, 1] * real_scale
    return jnp.stack([real_part, imag_part], axis=2)


def product(left, right):
    real_part = jnp.sum(
        left[:, :, 0] * right[:, :, 0] + left[:, :, 1] * right[:, :, 1], axis=(1, 2, 3, 4)
    )
    imag_part = jnp.sum(
        left[:, :, 0] * right[:, :, 1] - left[:, :, 1] * right[:, :, 0], axis=(1, 2, 3, 4)
    )
    return jnp.stack([real_part, imag_part])


def complex_times(first, other):
    return jnp.stack(
        [first[0] * other[0] - first[1] * other[1], first[0] * other[1] + first[1] * other[0]]
    )


def complex_ratio(first, other):
    modulus = other[0] * other[0] + other[1] * other[1]
    return (
        jnp.stack(
            [first[0] * other[0] + first[1] * other[1], first[1] * other[0] - first[0] * other[1]]
        )
        / modulus
    )


def grid_points(start, first, count):
    return (start + jnp.arange(first, count, dtype=jnp.int32)).astype(jnp.float32)


def body(source, permittivity, frequency):
    cells_x = source.shape[3]
    cells_y = source.shape[4]
    total_x = cells_x * lax.axis_size("gx")
    total_y = cells_y * lax.axis_size("gy")
    index_x = lax.axis_index("gx")
    index_y = lax.axis_index("gy")
    margin = 0
    front_x = orient(
        stretch(grid_points(index_x * cells_x, -margin, cells_x) + 0.5, total_x, frequency), 2
    )
    front_y = orient(
        stretch(grid_points(index_y * cells_y, -margin, cells_y) + 0.5, total_y, frequency), 3
    )
    back_x = orient(stretch(grid_points(index_x * cells_x, 0, cells_x), total_x, frequency), 2)
    back_y = orient(stretch(grid_points(index_y * cells_y, 0, cells_y), total_y, frequency), 3)
    z_points = grid_points(0, 0, NZ)
    front_z = orient(stretch(z_points + 0.5, NZ, frequency), 4)
    back_z = orient(stretch(z_points, NZ, frequency), 4)
    material = (frequency * frequency).reshape(-1, 1, 1, 1, 1, 1) * permittivity[None, :, None]

    def operate(values):
        above_x = shifted(values[:, :, :, :1], "gx", -1)
        above_y = shifted(values[:, :, :, :, :1], "gy", -1)
        extended = jnp.concatenate([values, above_x], axis=3)
        side_cells = jnp.concatenate([above_y, jnp.zeros_like(above_y[:, :, :, :1])], axis=3)
        extended = jnp.concatenate([extended, side_cells], axis=4)
        rotated = curl_forward(extended, front_x, front_y, front_z)
        below_x = shifted(rotated[:, :, :, -1:], "gx", 1)
        below_y = shifted(rotated[:, :, :, :, -1:], "gy", 1)
        padded = jnp.concatenate([below_x, rotated], axis=3)
        side_cells = jnp.concatenate([jnp.zeros_like(below_y[:, :, :, :1]), below_y], axis=3)
        padded = jnp.concatenate([side_cells, padded], axis=4)
        applied = curl_backward(padded, back_x, back_y, back_z)
        return applied - material * values

    solution = jnp.zeros_like(source)
    residual = source
    direction = source
    shadow_dot = lax.psum(product(source, residual), ("gx", "gy"))
    for iteration in range(ITERS):
        applied = operate(direction)
        step_size = complex_ratio(shadow_dot, lax.psum(product(source, applied), ("gx", "gy")))
        middle = residual - scaled(applied, step_size)
        second = operate(middle)
        sums_triple = lax.psum(
            (product(second, middle), product(second, second), product(source, second)),
            ("gx", "gy"),
        )
        weight = complex_ratio(sums_triple[0], sums_triple[1])
        solution = solution + scaled(direction, step_size) + scaled(middle, weight)
        residual = middle - scaled(second, weight)
        if iteration + 1 < ITERS:
            shadow_next = -complex_times(weight, sums_triple[2])
            momentum = complex_times(
                complex_ratio(shadow_next, shadow_dot), complex_ratio(step_size, weight)
            )
            direction = residual + scaled(direction - scaled(applied, weight), momentum)
            shadow_dot = shadow_next
    return (solution, residual)


def solution(mesh):
    placed = (P("groups", None, None, "gx", "gy", None), P("groups", "gx", "gy", None), P())
    return jax.shard_map(
        body,
        mesh=mesh,
        in_specs=placed,
        out_specs=(
            P("groups", None, None, "gx", "gy", None),
            P("groups", None, None, "gx", "gy", None),
        ),
        check_vma=False,
    )
```

profile of v0, /device:TPU:0, one launch (start us, length us, event | category | flops | bytes accessed | tf_op | source)
XLA Modules:
  0.0 469.3 jit_solution(13969787863053648633)
XLA Ops:
  1.6 1.3 collective-permute-start.1
  3.9 1.3 collective-permute-start
  7.5 6.7 %collective-permute-done = f32[1,3,2,1,32,256]{5,4,3,2,1,0:T(8,128)S(1)} collective-permute-done((f32[1,3,2,1,32,256]{5,4,3,2,1,0:T(8,128)S(1)}, f32[1,3,2,1,32,256]{5,4,3,2,1,0:T(8,128)S(1)}, u32[]{:S(2)}, u32[]{:S(2)}) %collective-permute-start) | collective-permute-done | bytes 196640 | tf_op jit(solution)/shard_map/ppermute | solution.py:15
  15.4 2.2 collective-permute-start.2
  17.5 5.0 %collective-permute-start.3 = (f32[1,3,2,1,32,256]{5,4,3,2,1,0:T(8,128)S(1)}, f32[1,3,2,1,32,256]{5,4,3,2,1,0:T(8,128)S(1)}, u32[]{:S(2)}, u32[]{:S(2)}) collective-permute-start(f32[1,3,2,1,32,256]{5,4,3,2,1,0:T(8,128)S(1)} %pad_maximum_fusion.33), channel_id=1, source_target_pairs={{0,2},{2,4},{4,6},{6,8},{8,10},{10,12},{12,14},{1,3},{3,5},{5,7},{... | collective-permute-start | bytes 589832 | tf_op jit(solution)/shard_map/ppermute | solution.py:15
  22.5 3.6 collective-permute-done.3
  29.7 1.4 pad_maximum_fusion.41
  31.1 31.3 %all-reduce.39 = (f32[2,1]{1,0:T(2,128)S(1)}, f32[2,1]{1,0:T(2,128)S(1)}) all-reduce(f32[2,1]{1,0:T(2,128)S(1)} %pad_maximum_fusion.41, f32[2,1]{1,0:T(2,128)S(1)} %pad_maximum_fusion.42), channel_id=1, replica_groups=mesh['groups'=2,'gx'=8,'gy'=2] {'gx','gy'}, use_global_device_ids=true, to_apply=%region_2.0 | all-reduce | flops 4 | bytes 32 | tf_op jit(solution)/shard_map/psum | solution.py:154
  71.5 1.3 multiply_subtract_fusion.14
  73.0 1.3 collective-permute-start.4
  74.3 1.3 collective-permute-start.5
  75.6 1.8 collective-permute-done.5
  77.4 3.2 collective-permute-done.4
  81.7 1.5 collective-permute-start.7
  83.2 1.7 collective-permute-start.6
  91.1 1.3 pad_maximum_fusion.45
  94.9 29.5 %all-reduce.38 = (f32[2,1]{1,0:T(2,128)S(1)}, f32[2,1]{1,0:T(2,128)S(1)}, f32[2,1]{1,0:T(2,128)S(1)}) all-reduce(f32[2,1]{1,0:T(2,128)S(1)} %pad_maximum_fusion.43, f32[2,1]{1,0:T(2,128)S(1)} %pad_maximum_fusion.44, f32[2,1]{1,0:T(2,128)S(1)} %pad_maximum_fusion.45), channel_id=1, replica_groups=mesh['groups'=2,'gx'=8,'gy'=2] {'gx','gy'}, use_global_device_ids=true, to_apply=%region_8.0 | all-reduce | flops 6 | bytes 48 | tf_op jit(solution)/shard_map/psum | solution.py:160
  141.5 2.5 multiply_subtract_fusion.11
  144.0 1.4 multiply_subtract_fusion.12
  163.9 1.3 collective-permute-start.8
  165.2 1.3 collective-permute-start.9
  166.5 1.8 collective-permute-done.9
  168.3 4.2 collective-permute-done.8
  173.6 1.5 collective-permute-start.11
  182.1 1.3 pad_maximum_fusion.46
  183.4 30.3 %psum.89 = f32[2,1]{1,0:T(2,128)S(1)} all-reduce(f32[2,1]{1,0:T(2,128)S(1)} %pad_maximum_fusion.46), channel_id=1, replica_groups=mesh['groups'=2,'gx'=8,'gy'=2] {'gx','gy'}, use_global_device_ids=true, to_apply=%region_17.0 | all-reduce | flops 2 | bytes 16 | tf_op jit(solution)/shard_map/psum | solution.py:157
  222.7 2.5 multiply_subtract_fusion.8
  225.6 1.3 collective-permute-start.12
  226.9 1.5 collective-permute-start.13
  228.4 1.6 collective-permute-done.13
  230.0 3.4 collective-permute-done.12
  235.0 1.5 collective-permute-start.15
  236.5 1.5 collective-permute-start.14
  245.7 1.8 pad_maximum_fusion.49
  247.5 1.9 pad_maximum_fusion.48
  249.4 1.9 pad_maximum_fusion.47
  251.3 30.6 %all-reduce.37 = (f32[2,1]{1,0:T(2,128)}, f32[2,1]{1,0:T(2,128)}, f32[2,1]{1,0:T(2,128)}) all-reduce(f32[2,1]{1,0:T(2,128)} %pad_maximum_fusion.47, f32[2,1]{1,0:T(2,128)} %pad_maximum_fusion.48, f32[2,1]{1,0:T(2,128)} %pad_maximum_fusion.49), channel_id=1, replica_groups=mesh['groups'=2,'gx'=8,'gy'=2] {'gx','gy'}, use_global_device_ids=true, to_apply=%region_20.0 | all-reduce | flops 6 | bytes 48 | tf_op jit(solution)/shard_map/psum | solution.py:160
  281.9 1.3 fusion.88
  283.2 1.3 fusion.87
  300.1 2.5 multiply_subtract_fusion.5
  323.3 1.3 collective-permute-start.16
  325.9 1.8 collective-permute-done.17
  327.7 3.7 collective-permute-done.16
  333.0 1.5 collective-permute-start.19
  336.7 1.7 collective-permute-done.19
  342.3 3.0 add_reduce_fusion.2
  345.3 1.8 pad_maximum_fusion.50
  347.1 2.3 multiply_subtract_fusion.13
  349.4 30.0 %psum.93 = f32[2,1]{1,0:T(2,128)S(1)} all-reduce(f32[2,1]{1,0:T(2,128)} %pad_maximum_fusion.50), channel_id=1, replica_groups=mesh['groups'=2,'gx'=8,'gy'=2] {'gx','gy'}, use_global_device_ids=true, to_apply=%region_29.0 | all-reduce | flops 2 | bytes 16 | tf_op jit(solution)/shard_map/psum | solution.py:157
  388.2 2.5 multiply_subtract_fusion.2
  390.7 2.3 maximum_subtract_fusion.11
  393.0 1.3 collective-permute-start.21
  394.3 1.3 collective-permute-start.20
  395.6 2.3 multiply_subtract_fusion.9
  397.9 5.9 %collective-permute-done.20 = f32[1,3,2,1,32,256]{5,4,3,2,1,0:T(8,128)S(1)} collective-permute-done((f32[1,3,2,1,32,256]{5,4,3,2,1,0:T(8,128)S(1)}, f32[1,3,2,1,32,256]{5,4,3,2,1,0:T(8,128)S(1)}, u32[]{:S(2)}, u32[]{:S(2)}) %collective-permute-start.20) | collective-permute-done | bytes 196640 | tf_op jit(solution)/shard_map/ppermute | solution.py:15
  405.4 2.0 collective-permute-start.22
  407.5 1.9 collective-permute-start.23
  409.3 2.2 multiply_subtract_fusion.7
  420.7 2.2 multiply_subtract_fusion.3
  422.9 29.5 %all-reduce.36 = (f32[2,1]{1,0:T(2,128)S(1)}, f32[2,1]{1,0:T(2,128)S(1)}) all-reduce(f32[2,1]{1,0:T(2,128)S(1)} %pad_maximum_fusion.51, f32[2,1]{1,0:T(2,128)S(1)} %pad_maximum_fusion.52), channel_id=1, replica_groups=mesh['groups'=2,'gx'=8,'gy'=2] {'gx','gy'}, use_global_device_ids=true, to_apply=%region_32.0 | all-reduce | flops 4 | bytes 32 | tf_op jit(solution)/shard_map/psum | solution.py:160
  461.4 2.6 multiply_subtract_fusion
  464.1 1.4 multiply_subtract_fusion.1
  465.6 1.5 maximum_subtract_fusion.13
  467.9 1.4 fusion.3
  (423 shorter events, 66.4 us)
Async XLA Ops:
  0.6 6.7 %copy-start.52 = (f32[3,4,32,256]{3,2,1,0:T(8,128)S(1)}, f32[3,4,32,256]{3,2,1,0:T(8,128)}, u32[]{:S(2)}) copy-start(f32[3,4,32,256]{3,2,1,0:T(8,128)} %param.4) | copy-start | bytes 1179652
  1.6 12.5 %collective-permute-start.1 = (f32[1,3,2,4,1,256]{5,4,3,2,1,0:T(1,128)S(1)}, f32[1,3,2,4,1,256]{5,4,3,2,1,0:T(1,128)S(1)}, u32[]{:S(2)}, u32[]{:S(2)}) collective-permute-start(f32[1,3,2,4,1,256]{5,4,3,2,1,0:T(1,128)S(1)} %slice.702), channel_id=1, source_target_pairs={{1,0},{3,2},{5,4},{7,6},{9,8},{11,10},{13,12},{15,14},{17,16},{19,... | collective-permute-start | bytes 73736 | tf_op jit(solution)/shard_map/ppermute | solution.py:15
  3.9 10.2 %collective-permute-start = (f32[1,3,2,1,32,256]{5,4,3,2,1,0:T(8,128)S(1)}, f32[1,3,2,1,32,256]{5,4,3,2,1,0:T(8,128)S(1)}, u32[]{:S(2)}, u32[]{:S(2)}) collective-permute-start(f32[1,3,2,1,32,256]{5,4,3,2,1,0:T(8,128)S(1)} %slice.695), channel_id=1, source_target_pairs={{2,0},{4,2},{6,4},{8,6},{10,8},{12,10},{14,12},{3,1},{5,3},{7,5},{... | collective-permute-start | bytes 589832 | tf_op jit(solution)/shard_map/ppermute | solution.py:15
  7.1 172.1 %copy-start.53 = (f32[4]{0:T(128)}, f32[4]{0:T(128)S(1)}, u32[]{:S(2)}) copy-start(f32[4]{0:T(128)S(1)} %get-tuple-element.424) | copy-start | bytes 52
  7.1 172.1 %copy-start.57 = (f32[4]{0:T(128)}, f32[4]{0:T(128)S(1)}, u32[]{:S(2)}) copy-start(f32[4]{0:T(128)S(1)} %get-tuple-element.425) | copy-start | bytes 52
  7.2 166.2 %copy-start.61 = (f32[4]{0:T(128)}, f32[4]{0:T(128)S(1)}, u32[]{:S(2)}) copy-start(f32[4]{0:T(128)S(1)} %get-tuple-element.432) | copy-start | bytes 52
  7.2 166.2 %copy-start.65 = (f32[4]{0:T(128)}, f32[4]{0:T(128)S(1)}, u32[]{:S(2)}) copy-start(f32[4]{0:T(128)S(1)} %get-tuple-element.433) | copy-start | bytes 52
  7.4 172.3 %copy-start.16 = (f32[3,4,32,256]{3,2,1,0:T(8,128)}, f32[3,4,32,256]{3,2,1,0:T(8,128)S(1)}, u32[]{:S(2)}) copy-start(f32[3,4,32,256]{3,2,1,0:T(8,128)S(1)} %broadcast_multiply_fusion) | copy-start | bytes 1179652
  7.4 165.7 %copy-start.77 = (f32[32]{0:T(128)}, f32[32]{0:T(128)S(1)}, u32[]{:S(2)}) copy-start(f32[32]{0:T(128)S(1)} %get-tuple-element.430) | copy-start | bytes 388
  7.4 165.7 %copy-start.81 = (f32[32]{0:T(128)}, f32[32]{0:T(128)S(1)}, u32[]{:S(2)}) copy-start(f32[32]{0:T(128)S(1)} %get-tuple-element.431) | copy-start | bytes 388
  7.4 6.8 %copy-start = (f32[1,3,2,4,32,256]{5,4,3,2,1,0:T(8,128)S(1)}, f32[1,3,2,4,32,256]{5,4,3,2,1,0:T(8,128)}, u32[]{:S(2)}) copy-start(f32[1,3,2,4,32,256]{5,4,3,2,1,0:T(8,128)} %param.3) | copy-start | bytes 2359300
  15.4 7.2 %collective-permute-start.2 = (f32[1,3,2,4,1,256]{5,4,3,2,1,0:T(1,128)S(1)}, f32[1,3,2,4,1,256]{5,4,3,2,1,0:T(1,128)S(1)}, u32[]{:S(2)}, u32[]{:S(2)}) collective-permute-start(f32[1,3,2,4,1,256]{5,4,3,2,1,0:T(1,128)S(1)} %pad_maximum_fusion.40), channel_id=1, source_target_pairs={{0,1},{2,3},{4,5},{6,7},{8,9},{10,11},{12,13},{14,15},{16,17},{18,... | collective-permute-start | bytes 73736 | tf_op jit(solution)/shard_map/ppermute | solution.py:15
  17.5 8.7 %collective-permute-start.3 = (f32[1,3,2,1,32,256]{5,4,3,2,1,0:T(8,128)S(1)}, f32[1,3,2,1,32,256]{5,4,3,2,1,0:T(8,128)S(1)}, u32[]{:S(2)}, u32[]{:S(2)}) collective-permute-start(f32[1,3,2,1,32,256]{5,4,3,2,1,0:T(8,128)S(1)} %pad_maximum_fusion.33), channel_id=1, source_target_pairs={{0,2},{2,4},{4,6},{6,8},{8,10},{10,12},{12,14},{1,3},{3,5},{5,7},{... | collective-permute-start | bytes 589832 | tf_op jit(solution)/shard_map/ppermute | solution.py:15
  22.5 156.8 %copy-start.69 = (f32[32]{0:T(128)}, f32[32]{0:T(128)S(1)}, u32[]{:S(2)}) copy-start(f32[32]{0:T(128)S(1)} %get-tuple-element.422) | copy-start | bytes 388
  22.5 156.8 %copy-start.73 = (f32[32]{0:T(128)}, f32[32]{0:T(128)S(1)}, u32[]{:S(2)}) copy-start(f32[32]{0:T(128)S(1)} %get-tuple-element.423) | copy-start | bytes 388
  27.5 45.4 %copy-start.27 = (f32[1,3,2,4,32,256]{5,4,3,2,1,0:T(8,128)}, f32[1,3,2,4,32,256]{5,4,3,2,1,0:T(8,128)S(1)}, u32[]{:S(2)}) copy-start(f32[1,3,2,4,32,256]{5,4,3,2,1,0:T(8,128)S(1)} %maximum_subtract_fusion) | copy-start | bytes 2359300
  73.0 7.6 %collective-permute-start.4 = (f32[1,3,2,1,32,256]{5,4,3,2,1,0:T(8,128)S(1)}, f32[1,3,2,1,32,256]{5,4,3,2,1,0:T(8,128)S(1)}, u32[]{:S(2)}, u32[]{:S(2)}) collective-permute-start(f32[1,3,2,1,32,256]{5,4,3,2,1,0:T(8,128)S(1)} %slice.2127), channel_id=1, source_target_pairs={{2,0},{4,2},{6,4},{8,6},{10,8},{12,10},{14,12},{3,1},{5,3},{7,5},{... | collective-permute-start | bytes 589832 | tf_op jit(solution)/shard_map/ppermute | solution.py:15
  74.3 3.1 collective-permute-start.5
  81.7 5.9 %collective-permute-start.7 = (f32[1,3,2,1,32,256]{5,4,3,2,1,0:T(8,128)S(1)}, f32[1,3,2,1,32,256]{5,4,3,2,1,0:T(8,128)S(1)}, u32[]{:S(2)}, u32[]{:S(2)}) collective-permute-start(f32[1,3,2,1,32,256]{5,4,3,2,1,0:T(8,128)S(1)} %pad_maximum_fusion.31), channel_id=1, source_target_pairs={{0,2},{2,4},{4,6},{6,8},{8,10},{10,12},{12,14},{1,3},{3,5},{5,7},{... | collective-permute-start | bytes 589832 | tf_op jit(solution)/shard_map/ppermute | solution.py:15
  83.2 4.4 collective-permute-start.6
  124.4 19.6 %copy-start.29 = (f32[1,3,2,4,32,256]{5,4,3,2,1,0:T(8,128)S(1)}, f32[1,3,2,4,32,256]{5,4,3,2,1,0:T(8,128)}, u32[]{:S(2)}) copy-start(f32[1,3,2,4,32,256]{5,4,3,2,1,0:T(8,128)} %copy-done.28) | copy-start | bytes 2359300
  145.4 34.3 %copy-start.1 = (f32[1,3,1,4,32,256]{5,4,3,2,1,0:T(8,128)}, f32[1,3,1,4,32,256]{5,4,3,2,1,0:T(8,128)S(1)}, u32[]{:S(2)}) copy-start(f32[1,3,1,4,32,256]{5,4,3,2,1,0:T(8,128)S(1)} %get-tuple-element.131) | copy-start | bytes 1179652
  163.5 16.2 %copy-start.34 = (f32[1,3,1,4,32,256]{5,4,3,2,1,0:T(8,128)}, f32[1,3,1,4,32,256]{5,4,3,2,1,0:T(8,128)S(1)}, u32[]{:S(2)}) copy-start(f32[1,3,1,4,32,256]{5,4,3,2,1,0:T(8,128)S(1)} %get-tuple-element.132) | copy-start | bytes 1179652
  163.5 16.2 %copy-start.36 = (f32[1,3,1,4,32,256]{5,4,3,2,1,0:T(8,128)}, f32[1,3,1,4,32,256]{5,4,3,2,1,0:T(8,128)S(1)}, u32[]{:S(2)}) copy-start(f32[1,3,1,4,32,256]{5,4,3,2,1,0:T(8,128)S(1)} %get-tuple-element.133) | copy-start | bytes 1179652
  163.9 9.1 %copy-start.5 = (f32[1,3,2,4,32,256]{5,4,3,2,1,0:T(8,128)}, f32[1,3,2,4,32,256]{5,4,3,2,1,0:T(8,128)S(1)}, u32[]{:S(2)}) copy-start(f32[1,3,2,4,32,256]{5,4,3,2,1,0:T(8,128)S(1)} %maximum_add_fusion.1) | copy-start | bytes 2359300
  163.9 8.6 %collective-permute-start.8 = (f32[1,3,2,1,32,256]{5,4,3,2,1,0:T(8,128)S(1)}, f32[1,3,2,1,32,256]{5,4,3,2,1,0:T(8,128)S(1)}, u32[]{:S(2)}, u32[]{:S(2)}) collective-permute-start(f32[1,3,2,1,32,256]{5,4,3,2,1,0:T(8,128)S(1)} %slice.2170), channel_id=1, source_target_pairs={{2,0},{4,2},{6,4},{8,6},{10,8},{12,10},{14,12},{3,1},{5,3},{7,5},{... | collective-permute-start | bytes 589832 | tf_op jit(solution)/shard_map/ppermute | solution.py:15
  165.2 3.1 collective-permute-start.9
  173.6 4.9 %collective-permute-start.11 = (f32[1,3,2,1,32,256]{5,4,3,2,1,0:T(8,128)S(1)}, f32[1,3,2,1,32,256]{5,4,3,2,1,0:T(8,128)S(1)}, u32[]{:S(2)}, u32[]{:S(2)}) collective-permute-start(f32[1,3,2,1,32,256]{5,4,3,2,1,0:T(8,128)S(1)} %pad_maximum_fusion.29), channel_id=1, source_target_pairs={{0,2},{2,4},{4,6},{6,8},{8,10},{10,12},{12,14},{1,3},{3,5},{5,7},{... | collective-permute-start | bytes 589832 | tf_op jit(solution)/shard_map/ppermute | solution.py:15
  175.1 2.1 collective-permute-start.10
  213.7 11.6 %copy-start.2 = (f32[1,3,1,4,32,256]{5,4,3,2,1,0:T(8,128)S(1)}, f32[1,3,1,4,32,256]{5,4,3,2,1,0:T(8,128)}, u32[]{:S(2)}) copy-start(f32[1,3,1,4,32,256]{5,4,3,2,1,0:T(8,128)} %copy-done.1) | copy-start | bytes 1179652
  225.2 17.0 %copy-start.9 = (f32[1,3,1,4,32,256]{5,4,3,2,1,0:T(8,128)}, f32[1,3,1,4,32,256]{5,4,3,2,1,0:T(8,128)S(1)}, u32[]{:S(2)}) copy-start(f32[1,3,1,4,32,256]{5,4,3,2,1,0:T(8,128)S(1)} %get-tuple-element.118) | copy-start | bytes 1179652
  225.2 17.0 %copy-start.12 = (f32[1,3,1,4,32,256]{5,4,3,2,1,0:T(8,128)}, f32[1,3,1,4,32,256]{5,4,3,2,1,0:T(8,128)S(1)}, u32[]{:S(2)}) copy-start(f32[1,3,1,4,32,256]{5,4,3,2,1,0:T(8,128)S(1)} %get-tuple-element.119) | copy-start | bytes 1179652
  225.6 7.8 %collective-permute-start.12 = (f32[1,3,2,1,32,256]{5,4,3,2,1,0:T(8,128)S(1)}, f32[1,3,2,1,32,256]{5,4,3,2,1,0:T(8,128)S(1)}, u32[]{:S(2)}, u32[]{:S(2)}) collective-permute-start(f32[1,3,2,1,32,256]{5,4,3,2,1,0:T(8,128)S(1)} %slice.2211), channel_id=1, source_target_pairs={{2,0},{4,2},{6,4},{8,6},{10,8},{12,10},{14,12},{3,1},{5,3},{7,5},{... | collective-permute-start | bytes 589832 | tf_op jit(solution)/shard_map/ppermute | solution.py:15
  226.9 3.1 collective-permute-start.13
  235.0 5.6 %collective-permute-start.15 = (f32[1,3,2,1,32,256]{5,4,3,2,1,0:T(8,128)S(1)}, f32[1,3,2,1,32,256]{5,4,3,2,1,0:T(8,128)S(1)}, u32[]{:S(2)}, u32[]{:S(2)}) collective-permute-start(f32[1,3,2,1,32,256]{5,4,3,2,1,0:T(8,128)S(1)} %pad_maximum_fusion.27), channel_id=1, source_target_pairs={{0,2},{2,4},{4,6},{6,8},{8,10},{10,12},{12,14},{1,3},{3,5},{5,7},{... | collective-permute-start | bytes 589832 | tf_op jit(solution)/shard_map/ppermute | solution.py:15
  236.5 4.0 collective-permute-start.14
  281.9 20.7 %copy-start.31 = (f32[1,3,2,4,32,256]{5,4,3,2,1,0:T(8,128)S(1)}, f32[1,3,2,4,32,256]{5,4,3,2,1,0:T(8,128)}, u32[]{:S(2)}) copy-start(f32[1,3,2,4,32,256]{5,4,3,2,1,0:T(8,128)} %copy-done.30) | copy-start | bytes 2359300
  300.0 3.8 copy-start.85
  300.0 21.2 %copy-start.3 = (f32[1,3,1,4,32,256]{5,4,3,2,1,0:T(8,128)S(1)}, f32[1,3,1,4,32,256]{5,4,3,2,1,0:T(8,128)}, u32[]{:S(2)}) copy-start(f32[1,3,1,4,32,256]{5,4,3,2,1,0:T(8,128)} %copy-done.1) | copy-start | bytes 1179652
  300.0 21.2 %copy-start.35 = (f32[1,3,1,4,32,256]{5,4,3,2,1,0:T(8,128)S(1)}, f32[1,3,1,4,32,256]{5,4,3,2,1,0:T(8,128)}, u32[]{:S(2)}) copy-start(f32[1,3,1,4,32,256]{5,4,3,2,1,0:T(8,128)} %copy-done.34) | copy-start | bytes 1179652
  300.0 21.2 %copy-start.37 = (f32[1,3,1,4,32,256]{5,4,3,2,1,0:T(8,128)S(1)}, f32[1,3,1,4,32,256]{5,4,3,2,1,0:T(8,128)}, u32[]{:S(2)}) copy-start(f32[1,3,1,4,32,256]{5,4,3,2,1,0:T(8,128)} %copy-done.36) | copy-start | bytes 1179652
  303.8 36.1 %copy-start.20 = (f32[1,3,1,4,32,256]{5,4,3,2,1,0:T(8,128)}, f32[1,3,1,4,32,256]{5,4,3,2,1,0:T(8,128)S(1)}, u32[]{:S(2)}) copy-start(f32[1,3,1,4,32,256]{5,4,3,2,1,0:T(8,128)S(1)} %get-tuple-element.100) | copy-start | bytes 1179652
  303.8 36.1 %copy-start.23 = (f32[1,3,1,4,32,256]{5,4,3,2,1,0:T(8,128)}, f32[1,3,1,4,32,256]{5,4,3,2,1,0:T(8,128)S(1)}, u32[]{:S(2)}) copy-start(f32[1,3,1,4,32,256]{5,4,3,2,1,0:T(8,128)S(1)} %get-tuple-element.101) | copy-start | bytes 1179652
  323.2 8.7 %copy-start.7 = (f32[1,3,2,4,32,256]{5,4,3,2,1,0:T(8,128)}, f32[1,3,2,4,32,256]{5,4,3,2,1,0:T(8,128)S(1)}, u32[]{:S(2)}) copy-start(f32[1,3,2,4,32,256]{5,4,3,2,1,0:T(8,128)S(1)} %maximum_add_fusion.2) | copy-start | bytes 2359300
  323.3 8.1 %collective-permute-start.16 = (f32[1,3,2,1,32,256]{5,4,3,2,1,0:T(8,128)S(1)}, f32[1,3,2,1,32,256]{5,4,3,2,1,0:T(8,128)S(1)}, u32[]{:S(2)}, u32[]{:S(2)}) collective-permute-start(f32[1,3,2,1,32,256]{5,4,3,2,1,0:T(8,128)S(1)} %slice.2254), channel_id=1, source_target_pairs={{2,0},{4,2},{6,4},{8,6},{10,8},{12,10},{14,12},{3,1},{5,3},{7,5},{... | collective-permute-start | bytes 589832 | tf_op jit(solution)/shard_map/ppermute | solution.py:15
  324.6 3.1 collective-permute-start.17
  333.0 5.3 %collective-permute-start.19 = (f32[1,3,2,1,32,256]{5,4,3,2,1,0:T(8,128)S(1)}, f32[1,3,2,1,32,256]{5,4,3,2,1,0:T(8,128)S(1)}, u32[]{:S(2)}, u32[]{:S(2)}) collective-permute-start(f32[1,3,2,1,32,256]{5,4,3,2,1,0:T(8,128)S(1)} %pad_maximum_fusion.25), channel_id=1, source_target_pairs={{0,2},{2,4},{4,6},{6,8},{8,10},{10,12},{12,14},{1,3},{3,5},{5,7},{... | collective-permute-start | bytes 589832 | tf_op jit(solution)/shard_map/ppermute | solution.py:15
  334.6 2.1 collective-permute-start.18
  390.6 23.8 %copy-start.38 = (f32[1,3,1,4,32,256]{5,4,3,2,1,0:T(8,128)}, f32[1,3,1,4,32,256]{5,4,3,2,1,0:T(8,128)S(1)}, u32[]{:S(2)}) copy-start(f32[1,3,1,4,32,256]{5,4,3,2,1,0:T(8,128)S(1)} %get-tuple-element.86) | copy-start | bytes 1179652
  390.7 23.8 %copy-start.40 = (f32[1,3,1,4,32,256]{5,4,3,2,1,0:T(8,128)}, f32[1,3,1,4,32,256]{5,4,3,2,1,0:T(8,128)S(1)}, u32[]{:S(2)}) copy-start(f32[1,3,1,4,32,256]{5,4,3,2,1,0:T(8,128)S(1)} %get-tuple-element.87) | copy-start | bytes 1179652
  390.7 4.9 %copy-start.6 = (f32[1,3,2,4,32,256]{5,4,3,2,1,0:T(8,128)S(1)}, f32[1,3,2,4,32,256]{5,4,3,2,1,0:T(8,128)}, u32[]{:S(2)}) copy-start(f32[1,3,2,4,32,256]{5,4,3,2,1,0:T(8,128)} %copy-done.5) | copy-start | bytes 2359300
  393.0 5.0 %collective-permute-start.21 = (f32[1,3,2,4,1,256]{5,4,3,2,1,0:T(1,128)S(1)}, f32[1,3,2,4,1,256]{5,4,3,2,1,0:T(1,128)S(1)}, u32[]{:S(2)}, u32[]{:S(2)}) collective-permute-start(f32[1,3,2,4,1,256]{5,4,3,2,1,0:T(1,128)S(1)} %slice.2299), channel_id=1, source_target_pairs={{1,0},{3,2},{5,4},{7,6},{9,8},{11,10},{13,12},{15,14},{17,16},{19,... | collective-permute-start | bytes 73736 | tf_op jit(solution)/shard_map/ppermute | solution.py:15
  394.3 9.5 %collective-permute-start.20 = (f32[1,3,2,1,32,256]{5,4,3,2,1,0:T(8,128)S(1)}, f32[1,3,2,1,32,256]{5,4,3,2,1,0:T(8,128)S(1)}, u32[]{:S(2)}, u32[]{:S(2)}) collective-permute-start(f32[1,3,2,1,32,256]{5,4,3,2,1,0:T(8,128)S(1)} %slice.2295), channel_id=1, source_target_pairs={{2,0},{4,2},{6,4},{8,6},{10,8},{12,10},{14,12},{3,1},{5,3},{7,5},{... | collective-permute-start | bytes 589832 | tf_op jit(solution)/shard_map/ppermute | solution.py:15
  405.4 6.1 %collective-permute-start.22 = (f32[1,3,2,4,1,256]{5,4,3,2,1,0:T(1,128)S(1)}, f32[1,3,2,4,1,256]{5,4,3,2,1,0:T(1,128)S(1)}, u32[]{:S(2)}, u32[]{:S(2)}) collective-permute-start(f32[1,3,2,4,1,256]{5,4,3,2,1,0:T(1,128)S(1)} %pad_maximum_fusion.35), channel_id=1, source_target_pairs={{0,1},{2,3},{4,5},{6,7},{8,9},{10,11},{12,13},{14,15},{16,17},{18,... | collective-permute-start | bytes 73736 | tf_op jit(solution)/shard_map/ppermute | solution.py:15
  407.5 5.3 %collective-permute-start.23 = (f32[1,3,2,1,32,256]{5,4,3,2,1,0:T(8,128)S(1)}, f32[1,3,2,1,32,256]{5,4,3,2,1,0:T(8,128)S(1)}, u32[]{:S(2)}, u32[]{:S(2)}) collective-permute-start(f32[1,3,2,1,32,256]{5,4,3,2,1,0:T(8,128)S(1)} %pad_maximum_fusion.23), channel_id=1, source_target_pairs={{0,2},{2,4},{4,6},{6,8},{8,10},{10,12},{12,14},{1,3},{3,5},{5,7},{... | collective-permute-start | bytes 589832 | tf_op jit(solution)/shard_map/ppermute | solution.py:15
  417.3 3.3 copy-start.8
  461.4 4.0 copy-start.15
  461.4 4.0 copy-start.22
  461.4 4.1 copy-start.25
  461.4 4.1 copy-start.39
  461.4 4.1 copy-start.41
  465.6 2.1 copy-start.49
  465.6 2.2 copy-start.50
  465.6 2.3 copy-start.51
  (46 other events, 43.2 us)
where the time goes:
time: 472 us; the launch traced here: 469 us
  blocking collectives  181 us (38%)
  between operations  99.9 us (21%)
  other arithmetic  74.5 us (16%)
  waiting for transfers between devices  43.6 us (9%)
  starting transfers between devices  38.4 us (8%)
  local copies, waits for them, and re-layouts  31.8 us (7%)
    psum x3, blocking collectives, body(): lax.psum((product(second, middle), product(second, second), product(sourc...  89.6 us
    psum x2, blocking collectives, body(): lax.psum(product(source, applied), ('gx', 'gy'))  60.3 us
    ppermute x24, waiting for transfers between devices, shifted(): return lax.ppermute(array, axis, pairs)  43.6 us
    ppermute x24, starting transfers between devices, shifted(): return lax.ppermute(array, axis, pairs)  38.4 us
    psum x1, blocking collectives, body(): shadow_dot = lax.psum(product(source, residual), ('gx', 'gy'))  31.3 us
    sub x15, other arithmetic, scaled(): real_part = values[:, :, 0] * real_scale - values[:, :, 1] * imag_scale  27.3 us
    another operation x12, other arithmetic, product(): return jnp.stack([real_part, imag_part])  17.5 us
    unnamed x173, local copies, waits for them, and re-layouts  12.9 us
  transfers between devices with their start and end apart: 24, of which 17 were waited for; matrix products, arithmetic and copies ran while one was open for 2% of the time, Pallas kernels for 0%

commit v1 on v0

--- a/solution.py
+++ b/solution.py
@@ -151,7 +151,7 @@
     solution = jnp.zeros_like(source)
     residual = source
     direction = source
-    shadow_dot = lax.psum(product(source, residual), ("gx", "gy"))
+    shadow_dot = lax.psum(lax.psum(product(source, residual), "gy"), "gx")
     for iteration in range(ITERS):
         applied = operate(direction)
         step_size = complex_ratio(shadow_dot, lax.psum(product(source, applied), ("gx", "gy")))

time: 472 us -> 493 us (1.044)
  blocking collectives: 181 us -> 201 us
    psum x2 -> x3, blocking collectives: 60.3 us -> 91.6 us  [body(): lax.psum(product(source, applied), ('gx', 'gy'))]
    psum x1 -> x2, blocking collectives: 31.3 us -> 19.6 us  [body(): shadow_dot = lax.psum(lax.psum(product(source, residual), 'gy'), 'gx')]
  transfers between devices with their start and end apart: 24 -> 24, of which waited for: 17 -> 17; matrix products, arithmetic and copies ran while one was open for 2% -> 1% of each run, Pallas kernels for 0% -> 0%
where the time goes in v1:
time: 493 us; the launch traced here: 490 us
  blocking collectives  201 us (41%)
  between operations  98 us (20%)
  other arithmetic  74.2 us (15%)
  waiting for transfers between devices  43.7 us (9%)
  starting transfers between devices  41.3 us (8%)
  local copies, waits for them, and re-layouts  31.6 us (6%)
    psum x3, blocking collectives, body(): lax.psum(product(source, applied), ('gx', 'gy'))  91.6 us
    psum x3, blocking collectives, body(): lax.psum((product(second, middle), product(second, second), product(sourc...  89.6 us
    ppermute x24, waiting for transfers between devices, shifted(): return lax.ppermute(array, axis, pairs)  43.7 us
    ppermute x24, starting transfers between devices, shifted(): return lax.ppermute(array, axis, pairs)  41.3 us
    sub x15, other arithmetic, scaled(): real_part = values[:, :, 0] * real_scale - values[:, :, 1] * imag_scale  27 us
    psum x2, blocking collectives, body(): shadow_dot = lax.psum(lax.psum(product(source, residual), 'gy'), 'gx')  19.6 us
    another operation x12, other arithmetic, product(): return jnp.stack([real_part, imag_part])  17.5 us
    unnamed x173, local copies, waits for them, and re-layouts  13 us
  transfers between devices with their start and end apart: 24, of which 17 were waited for; matrix products, arithmetic and copies ran while one was open for 1% of the time, Pallas kernels for 0%

profile of v1, /device:TPU:0, one launch (start us, length us, event | category | flops | bytes accessed | tf_op | source)
XLA Modules:
  0.0 489.5 jit_solution(8392014566516099603)
XLA Ops:
  1.6 1.3 collective-permute-start.1
  3.9 1.3 collective-permute-start
  7.5 6.7 %collective-permute-done = f32[1,3,2,1,32,256]{5,4,3,2,1,0:T(8,128)S(1)} collective-permute-done((f32[1,3,2,1,32,256]{5,4,3,2,1,0:T(8,128)S(1)}, f32[1,3,2,1,32,256]{5,4,3,2,1,0:T(8,128)S(1)}, u32[]{:S(2)}, u32[]{:S(2)}) %collective-permute-start) | collective-permute-done | bytes 196640 | tf_op jit(solution)/shard_map/ppermute | solution.py:15
  15.4 2.2 collective-permute-start.2
  17.5 5.0 %collective-permute-start.3 = (f32[1,3,2,1,32,256]{5,4,3,2,1,0:T(8,128)S(1)}, f32[1,3,2,1,32,256]{5,4,3,2,1,0:T(8,128)S(1)}, u32[]{:S(2)}, u32[]{:S(2)}) collective-permute-start(f32[1,3,2,1,32,256]{5,4,3,2,1,0:T(8,128)S(1)} %pad_maximum_fusion.33), channel_id=1, source_target_pairs={{0,2},{2,4},{4,6},{6,8},{8,10},{10,12},{12,14},{1,3},{3,5},{5,7},{... | collective-permute-start | bytes 589832 | tf_op jit(solution)/shard_map/ppermute | solution.py:15
  22.5 3.6 collective-permute-done.3
  29.8 31.3 %psum.93 = f32[2,1]{1,0:T(2,128)S(1)} all-reduce(f32[2,1]{1,0:T(2,128)S(1)} %pad_maximum_fusion.42), channel_id=1, replica_groups=mesh['groups'=2,'gx'=8,'gy'=2] {'gx','gy'}, use_global_device_ids=true, to_apply=%region_6.0 | all-reduce | flops 2 | bytes 16 | tf_op jit(solution)/shard_map/psum | solution.py:157
  64.1 2.5 psum.91
  67.9 17.1 %psum.92 = f32[2,1]{1,0:T(2,128)S(1)} all-reduce(f32[2,1]{1,0:T(2,128)S(1)} %psum.91), channel_id=1, replica_groups=mesh['groups'=2,'gx'=8,'gy'=2] {'gx'}, use_global_device_ids=true, to_apply=%region_3.0 | all-reduce | flops 2 | bytes 16 | tf_op jit(solution)/shard_map/psum | solution.py:154
  91.3 1.4 multiply_subtract_fusion.14
  92.9 1.3 collective-permute-start.4
  94.2 1.3 collective-permute-start.5
  95.5 1.8 collective-permute-done.5
  97.3 3.2 collective-permute-done.4
  101.6 4.8 collective-permute-start.7
  116.2 1.4 pad_maximum_fusion.43
  117.6 29.5 %all-reduce.38 = (f32[2,1]{1,0:T(2,128)S(1)}, f32[2,1]{1,0:T(2,128)S(1)}, f32[2,1]{1,0:T(2,128)S(1)}) all-reduce(f32[2,1]{1,0:T(2,128)S(1)} %pad_maximum_fusion.43, f32[2,1]{1,0:T(2,128)S(1)} %pad_maximum_fusion.44, f32[2,1]{1,0:T(2,128)S(1)} %pad_maximum_fusion.45), channel_id=1, replica_groups=mesh['groups'=2,'gx'=8,'gy'=2] {'gx','gy'}, use_global_device_ids=true, to_apply=%region_9.0 | all-reduce | flops 6 | bytes 48 | tf_op jit(solution)/shard_map/psum | solution.py:160
  163.1 2.4 multiply_subtract_fusion.11
  184.6 1.3 collective-permute-start.8
  185.9 1.3 collective-permute-start.9
  187.2 1.8 collective-permute-done.9
  189.0 4.2 collective-permute-done.8
  194.3 1.5 collective-permute-start.11
  204.0 30.3 %psum.97 = f32[2,1]{1,0:T(2,128)S(1)} all-reduce(f32[2,1]{1,0:T(2,128)S(1)} %pad_maximum_fusion.46), channel_id=1, replica_groups=mesh['groups'=2,'gx'=8,'gy'=2] {'gx','gy'}, use_global_device_ids=true, to_apply=%region_18.0 | all-reduce | flops 2 | bytes 16 | tf_op jit(solution)/shard_map/psum | solution.py:157
  242.9 2.5 multiply_subtract_fusion.8
  245.8 1.3 collective-permute-start.12
  247.1 1.5 collective-permute-start.13
  248.6 1.6 collective-permute-done.13
  250.2 3.4 collective-permute-done.12
  255.2 1.5 collective-permute-start.15
  256.7 1.5 collective-permute-start.14
  265.9 1.7 pad_maximum_fusion.49
  267.7 1.9 pad_maximum_fusion.48
  269.6 2.0 pad_maximum_fusion.47
  271.6 30.6 %all-reduce.37 = (f32[2,1]{1,0:T(2,128)}, f32[2,1]{1,0:T(2,128)}, f32[2,1]{1,0:T(2,128)}) all-reduce(f32[2,1]{1,0:T(2,128)} %pad_maximum_fusion.47, f32[2,1]{1,0:T(2,128)} %pad_maximum_fusion.48, f32[2,1]{1,0:T(2,128)} %pad_maximum_fusion.49), channel_id=1, replica_groups=mesh['groups'=2,'gx'=8,'gy'=2] {'gx','gy'}, use_global_device_ids=true, to_apply=%region_21.0 | all-reduce | flops 6 | bytes 48 | tf_op jit(solution)/shard_map/psum | solution.py:160
  302.2 1.3 fusion.88
  303.5 1.4 fusion.87
  320.6 2.5 multiply_subtract_fusion.5
  323.1 1.3 multiply_subtract_fusion.6
  343.7 1.3 collective-permute-start.16
  345.1 1.3 collective-permute-start.17
  346.4 1.8 collective-permute-done.17
  348.1 3.7 collective-permute-done.16
  353.5 1.5 collective-permute-start.19
  357.1 1.7 collective-permute-done.19
  362.8 3.0 add_reduce_fusion.2
  365.8 1.7 pad_maximum_fusion.50
  367.5 2.2 multiply_subtract_fusion.13
  369.7 30.0 %psum.101 = f32[2,1]{1,0:T(2,128)S(1)} all-reduce(f32[2,1]{1,0:T(2,128)} %pad_maximum_fusion.50), channel_id=1, replica_groups=mesh['groups'=2,'gx'=8,'gy'=2] {'gx','gy'}, use_global_device_ids=true, to_apply=%region_30.0 | all-reduce | flops 2 | bytes 16 | tf_op jit(solution)/shard_map/psum | solution.py:157
  408.2 2.5 multiply_subtract_fusion.2
  410.8 2.3 maximum_subtract_fusion.11
  415.7 2.3 multiply_subtract_fusion.9
  418.0 5.9 %collective-permute-done.20 = f32[1,3,2,1,32,256]{5,4,3,2,1,0:T(8,128)S(1)} collective-permute-done((f32[1,3,2,1,32,256]{5,4,3,2,1,0:T(8,128)S(1)}, f32[1,3,2,1,32,256]{5,4,3,2,1,0:T(8,128)S(1)}, u32[]{:S(2)}, u32[]{:S(2)}) %collective-permute-start.20) | collective-permute-done | bytes 196640 | tf_op jit(solution)/shard_map/ppermute | solution.py:15
  425.6 2.0 collective-permute-start.22
  427.6 1.9 collective-permute-start.23
  429.5 2.2 multiply_subtract_fusion.7
  438.5 1.3 pad_maximum_fusion.52
  439.8 1.3 pad_maximum_fusion.51
  441.1 2.3 multiply_subtract_fusion.3
  443.4 29.5 %all-reduce.36 = (f32[2,1]{1,0:T(2,128)S(1)}, f32[2,1]{1,0:T(2,128)S(1)}) all-reduce(f32[2,1]{1,0:T(2,128)S(1)} %pad_maximum_fusion.51, f32[2,1]{1,0:T(2,128)S(1)} %pad_maximum_fusion.52), channel_id=1, replica_groups=mesh['groups'=2,'gx'=8,'gy'=2] {'gx','gy'}, use_global_device_ids=true, to_apply=%region_33.0 | all-reduce | flops 4 | bytes 32 | tf_op jit(solution)/shard_map/psum | solution.py:160
  481.8 2.6 multiply_subtract_fusion
  484.4 1.3 multiply_subtract_fusion.1
  485.9 1.5 maximum_subtract_fusion.13
  488.2 1.4 fusion.3
  (425 shorter events, 69.0 us)
Async XLA Ops:
  0.6 6.7 %copy-start.52 = (f32[3,4,32,256]{3,2,1,0:T(8,128)S(1)}, f32[3,4,32,256]{3,2,1,0:T(8,128)}, u32[]{:S(2)}) copy-start(f32[3,4,32,256]{3,2,1,0:T(8,128)} %param.4) | copy-start | bytes 1179652
  1.6 12.5 %collective-permute-start.1 = (f32[1,3,2,4,1,256]{5,4,3,2,1,0:T(1,128)S(1)}, f32[1,3,2,4,1,256]{5,4,3,2,1,0:T(1,128)S(1)}, u32[]{:S(2)}, u32[]{:S(2)}) collective-permute-start(f32[1,3,2,4,1,256]{5,4,3,2,1,0:T(1,128)S(1)} %slice.702), channel_id=1, source_target_pairs={{1,0},{3,2},{5,4},{7,6},{9,8},{11,10},{13,12},{15,14},{17,16},{19,... | collective-permute-start | bytes 73736 | tf_op jit(solution)/shard_map/ppermute | solution.py:15
  3.9 10.2 %collective-permute-start = (f32[1,3,2,1,32,256]{5,4,3,2,1,0:T(8,128)S(1)}, f32[1,3,2,1,32,256]{5,4,3,2,1,0:T(8,128)S(1)}, u32[]{:S(2)}, u32[]{:S(2)}) collective-permute-start(f32[1,3,2,1,32,256]{5,4,3,2,1,0:T(8,128)S(1)} %slice.695), channel_id=1, source_target_pairs={{2,0},{4,2},{6,4},{8,6},{10,8},{12,10},{14,12},{3,1},{5,3},{7,5},{... | collective-permute-start | bytes 589832 | tf_op jit(solution)/shard_map/ppermute | solution.py:15
  7.1 192.8 %copy-start.53 = (f32[4]{0:T(128)}, f32[4]{0:T(128)S(1)}, u32[]{:S(2)}) copy-start(f32[4]{0:T(128)S(1)} %get-tuple-element.422) | copy-start | bytes 52
  7.1 192.8 %copy-start.57 = (f32[4]{0:T(128)}, f32[4]{0:T(128)S(1)}, u32[]{:S(2)}) copy-start(f32[4]{0:T(128)S(1)} %get-tuple-element.423) | copy-start | bytes 52
  7.2 186.9 %copy-start.61 = (f32[4]{0:T(128)}, f32[4]{0:T(128)S(1)}, u32[]{:S(2)}) copy-start(f32[4]{0:T(128)S(1)} %get-tuple-element.430) | copy-start | bytes 52
  7.2 186.9 %copy-start.65 = (f32[4]{0:T(128)}, f32[4]{0:T(128)S(1)}, u32[]{:S(2)}) copy-start(f32[4]{0:T(128)S(1)} %get-tuple-element.431) | copy-start | bytes 52
  7.4 193.0 %copy-start.16 = (f32[3,4,32,256]{3,2,1,0:T(8,128)}, f32[3,4,32,256]{3,2,1,0:T(8,128)S(1)}, u32[]{:S(2)}) copy-start(f32[3,4,32,256]{3,2,1,0:T(8,128)S(1)} %broadcast_multiply_fusion) | copy-start | bytes 1179652
  7.4 186.4 %copy-start.77 = (f32[32]{0:T(128)}, f32[32]{0:T(128)S(1)}, u32[]{:S(2)}) copy-start(f32[32]{0:T(128)S(1)} %get-tuple-element.428) | copy-start | bytes 388
  7.4 186.4 %copy-start.81 = (f32[32]{0:T(128)}, f32[32]{0:T(128)S(1)}, u32[]{:S(2)}) copy-start(f32[32]{0:T(128)S(1)} %get-tuple-element.429) | copy-start | bytes 388
  7.4 6.8 %copy-start = (f32[1,3,2,4,32,256]{5,4,3,2,1,0:T(8,128)S(1)}, f32[1,3,2,4,32,256]{5,4,3,2,1,0:T(8,128)}, u32[]{:S(2)}) copy-start(f32[1,3,2,4,32,256]{5,4,3,2,1,0:T(8,128)} %param.3) | copy-start | bytes 2359300
  15.4 7.2 %collective-permute-start.2 = (f32[1,3,2,4,1,256]{5,4,3,2,1,0:T(1,128)S(1)}, f32[1,3,2,4,1,256]{5,4,3,2,1,0:T(1,128)S(1)}, u32[]{:S(2)}, u32[]{:S(2)}) collective-permute-start(f32[1,3,2,4,1,256]{5,4,3,2,1,0:T(1,128)S(1)} %pad_maximum_fusion.40), channel_id=1, source_target_pairs={{0,1},{2,3},{4,5},{6,7},{8,9},{10,11},{12,13},{14,15},{16,17},{18,... | collective-permute-start | bytes 73736 | tf_op jit(solution)/shard_map/ppermute | solution.py:15
  17.5 8.7 %collective-permute-start.3 = (f32[1,3,2,1,32,256]{5,4,3,2,1,0:T(8,128)S(1)}, f32[1,3,2,1,32,256]{5,4,3,2,1,0:T(8,128)S(1)}, u32[]{:S(2)}, u32[]{:S(2)}) collective-permute-start(f32[1,3,2,1,32,256]{5,4,3,2,1,0:T(8,128)S(1)} %pad_maximum_fusion.33), channel_id=1, source_target_pairs={{0,2},{2,4},{4,6},{6,8},{8,10},{10,12},{12,14},{1,3},{3,5},{5,7},{... | collective-permute-start | bytes 589832 | tf_op jit(solution)/shard_map/ppermute | solution.py:15
  22.5 177.5 %copy-start.69 = (f32[32]{0:T(128)}, f32[32]{0:T(128)S(1)}, u32[]{:S(2)}) copy-start(f32[32]{0:T(128)S(1)} %get-tuple-element.420) | copy-start | bytes 388
  22.5 177.5 %copy-start.73 = (f32[32]{0:T(128)}, f32[32]{0:T(128)S(1)}, u32[]{:S(2)}) copy-start(f32[32]{0:T(128)S(1)} %get-tuple-element.421) | copy-start | bytes 388
  27.5 65.3 %copy-start.27 = (f32[1,3,2,4,32,256]{5,4,3,2,1,0:T(8,128)}, f32[1,3,2,4,32,256]{5,4,3,2,1,0:T(8,128)S(1)}, u32[]{:S(2)}) copy-start(f32[1,3,2,4,32,256]{5,4,3,2,1,0:T(8,128)S(1)} %maximum_subtract_fusion) | copy-start | bytes 2359300
  92.9 7.6 %collective-permute-start.4 = (f32[1,3,2,1,32,256]{5,4,3,2,1,0:T(8,128)S(1)}, f32[1,3,2,1,32,256]{5,4,3,2,1,0:T(8,128)S(1)}, u32[]{:S(2)}, u32[]{:S(2)}) collective-permute-start(f32[1,3,2,1,32,256]{5,4,3,2,1,0:T(8,128)S(1)} %slice.2127), channel_id=1, source_target_pairs={{2,0},{4,2},{6,4},{8,6},{10,8},{12,10},{14,12},{3,1},{5,3},{7,5},{... | collective-permute-start | bytes 589832 | tf_op jit(solution)/shard_map/ppermute | solution.py:15
  94.2 3.1 collective-permute-start.5
  101.6 8.7 %collective-permute-start.7 = (f32[1,3,2,1,32,256]{5,4,3,2,1,0:T(8,128)S(1)}, f32[1,3,2,1,32,256]{5,4,3,2,1,0:T(8,128)S(1)}, u32[]{:S(2)}, u32[]{:S(2)}) collective-permute-start(f32[1,3,2,1,32,256]{5,4,3,2,1,0:T(8,128)S(1)} %pad_maximum_fusion.31), channel_id=1, source_target_pairs={{0,2},{2,4},{4,6},{6,8},{8,10},{10,12},{12,14},{1,3},{3,5},{5,7},{... | collective-permute-start | bytes 589832 | tf_op jit(solution)/shard_map/ppermute | solution.py:15
  106.4 3.8 collective-permute-start.6
  147.1 18.5 %copy-start.29 = (f32[1,3,2,4,32,256]{5,4,3,2,1,0:T(8,128)S(1)}, f32[1,3,2,4,32,256]{5,4,3,2,1,0:T(8,128)}, u32[]{:S(2)}) copy-start(f32[1,3,2,4,32,256]{5,4,3,2,1,0:T(8,128)} %copy-done.28) | copy-start | bytes 2359300
  166.8 33.6 %copy-start.1 = (f32[1,3,1,4,32,256]{5,4,3,2,1,0:T(8,128)}, f32[1,3,1,4,32,256]{5,4,3,2,1,0:T(8,128)S(1)}, u32[]{:S(2)}) copy-start(f32[1,3,1,4,32,256]{5,4,3,2,1,0:T(8,128)S(1)} %get-tuple-element.129) | copy-start | bytes 1179652
  184.2 16.2 %copy-start.34 = (f32[1,3,1,4,32,256]{5,4,3,2,1,0:T(8,128)}, f32[1,3,1,4,32,256]{5,4,3,2,1,0:T(8,128)S(1)}, u32[]{:S(2)}) copy-start(f32[1,3,1,4,32,256]{5,4,3,2,1,0:T(8,128)S(1)} %get-tuple-element.130) | copy-start | bytes 1179652
  184.2 16.2 %copy-start.36 = (f32[1,3,1,4,32,256]{5,4,3,2,1,0:T(8,128)}, f32[1,3,1,4,32,256]{5,4,3,2,1,0:T(8,128)S(1)}, u32[]{:S(2)}) copy-start(f32[1,3,1,4,32,256]{5,4,3,2,1,0:T(8,128)S(1)} %get-tuple-element.131) | copy-start | bytes 1179652
  184.6 9.1 %copy-start.5 = (f32[1,3,2,4,32,256]{5,4,3,2,1,0:T(8,128)}, f32[1,3,2,4,32,256]{5,4,3,2,1,0:T(8,128)S(1)}, u32[]{:S(2)}) copy-start(f32[1,3,2,4,32,256]{5,4,3,2,1,0:T(8,128)S(1)} %maximum_add_fusion.1) | copy-start | bytes 2359300
  184.6 8.6 %collective-permute-start.8 = (f32[1,3,2,1,32,256]{5,4,3,2,1,0:T(8,128)S(1)}, f32[1,3,2,1,32,256]{5,4,3,2,1,0:T(8,128)S(1)}, u32[]{:S(2)}, u32[]{:S(2)}) collective-permute-start(f32[1,3,2,1,32,256]{5,4,3,2,1,0:T(8,128)S(1)} %slice.2170), channel_id=1, source_target_pairs={{2,0},{4,2},{6,4},{8,6},{10,8},{12,10},{14,12},{3,1},{5,3},{7,5},{... | collective-permute-start | bytes 589832 | tf_op jit(solution)/shard_map/ppermute | solution.py:15
  185.9 3.1 collective-permute-start.9
  194.3 4.9 collective-permute-start.11
  195.8 2.1 collective-permute-start.10
  234.3 11.1 %copy-start.2 = (f32[1,3,1,4,32,256]{5,4,3,2,1,0:T(8,128)S(1)}, f32[1,3,1,4,32,256]{5,4,3,2,1,0:T(8,128)}, u32[]{:S(2)}) copy-start(f32[1,3,1,4,32,256]{5,4,3,2,1,0:T(8,128)} %copy-done.1) | copy-start | bytes 1179652
  245.4 17.0 %copy-start.9 = (f32[1,3,1,4,32,256]{5,4,3,2,1,0:T(8,128)}, f32[1,3,1,4,32,256]{5,4,3,2,1,0:T(8,128)S(1)}, u32[]{:S(2)}) copy-start(f32[1,3,1,4,32,256]{5,4,3,2,1,0:T(8,128)S(1)} %get-tuple-element.116) | copy-start | bytes 1179652
  245.4 17.0 %copy-start.12 = (f32[1,3,1,4,32,256]{5,4,3,2,1,0:T(8,128)}, f32[1,3,1,4,32,256]{5,4,3,2,1,0:T(8,128)S(1)}, u32[]{:S(2)}) copy-start(f32[1,3,1,4,32,256]{5,4,3,2,1,0:T(8,128)S(1)} %get-tuple-element.117) | copy-start | bytes 1179652
  245.8 7.8 %collective-permute-start.12 = (f32[1,3,2,1,32,256]{5,4,3,2,1,0:T(8,128)S(1)}, f32[1,3,2,1,32,256]{5,4,3,2,1,0:T(8,128)S(1)}, u32[]{:S(2)}, u32[]{:S(2)}) collective-permute-start(f32[1,3,2,1,32,256]{5,4,3,2,1,0:T(8,128)S(1)} %slice.2211), channel_id=1, source_target_pairs={{2,0},{4,2},{6,4},{8,6},{10,8},{12,10},{14,12},{3,1},{5,3},{7,5},{... | collective-permute-start | bytes 589832 | tf_op jit(solution)/shard_map/ppermute | solution.py:15
  247.1 3.1 collective-permute-start.13
  255.2 5.6 %collective-permute-start.15 = (f32[1,3,2,1,32,256]{5,4,3,2,1,0:T(8,128)S(1)}, f32[1,3,2,1,32,256]{5,4,3,2,1,0:T(8,128)S(1)}, u32[]{:S(2)}, u32[]{:S(2)}) collective-permute-start(f32[1,3,2,1,32,256]{5,4,3,2,1,0:T(8,128)S(1)} %pad_maximum_fusion.27), channel_id=1, source_target_pairs={{0,2},{2,4},{4,6},{6,8},{8,10},{10,12},{12,14},{1,3},{3,5},{5,7},{... | collective-permute-start | bytes 589832 | tf_op jit(solution)/shard_map/ppermute | solution.py:15
  256.7 3.9 collective-permute-start.14
  302.2 21.0 %copy-start.31 = (f32[1,3,2,4,32,256]{5,4,3,2,1,0:T(8,128)S(1)}, f32[1,3,2,4,32,256]{5,4,3,2,1,0:T(8,128)}, u32[]{:S(2)}) copy-start(f32[1,3,2,4,32,256]{5,4,3,2,1,0:T(8,128)} %copy-done.30) | copy-start | bytes 2359300
  320.6 3.9 copy-start.85
  320.6 21.1 %copy-start.3 = (f32[1,3,1,4,32,256]{5,4,3,2,1,0:T(8,128)S(1)}, f32[1,3,1,4,32,256]{5,4,3,2,1,0:T(8,128)}, u32[]{:S(2)}) copy-start(f32[1,3,1,4,32,256]{5,4,3,2,1,0:T(8,128)} %copy-done.1) | copy-start | bytes 1179652
  320.6 21.1 %copy-start.35 = (f32[1,3,1,4,32,256]{5,4,3,2,1,0:T(8,128)S(1)}, f32[1,3,1,4,32,256]{5,4,3,2,1,0:T(8,128)}, u32[]{:S(2)}) copy-start(f32[1,3,1,4,32,256]{5,4,3,2,1,0:T(8,128)} %copy-done.34) | copy-start | bytes 1179652
  320.6 21.1 %copy-start.37 = (f32[1,3,1,4,32,256]{5,4,3,2,1,0:T(8,128)S(1)}, f32[1,3,1,4,32,256]{5,4,3,2,1,0:T(8,128)}, u32[]{:S(2)}) copy-start(f32[1,3,1,4,32,256]{5,4,3,2,1,0:T(8,128)} %copy-done.36) | copy-start | bytes 1179652
  324.4 36.0 %copy-start.20 = (f32[1,3,1,4,32,256]{5,4,3,2,1,0:T(8,128)}, f32[1,3,1,4,32,256]{5,4,3,2,1,0:T(8,128)S(1)}, u32[]{:S(2)}) copy-start(f32[1,3,1,4,32,256]{5,4,3,2,1,0:T(8,128)S(1)} %get-tuple-element.98) | copy-start | bytes 1179652
  324.4 36.0 %copy-start.23 = (f32[1,3,1,4,32,256]{5,4,3,2,1,0:T(8,128)}, f32[1,3,1,4,32,256]{5,4,3,2,1,0:T(8,128)S(1)}, u32[]{:S(2)}) copy-start(f32[1,3,1,4,32,256]{5,4,3,2,1,0:T(8,128)S(1)} %get-tuple-element.99) | copy-start | bytes 1179652
  343.7 8.7 %copy-start.7 = (f32[1,3,2,4,32,256]{5,4,3,2,1,0:T(8,128)}, f32[1,3,2,4,32,256]{5,4,3,2,1,0:T(8,128)S(1)}, u32[]{:S(2)}) copy-start(f32[1,3,2,4,32,256]{5,4,3,2,1,0:T(8,128)S(1)} %maximum_add_fusion.2) | copy-start | bytes 2359300
  343.7 8.1 %collective-permute-start.16 = (f32[1,3,2,1,32,256]{5,4,3,2,1,0:T(8,128)S(1)}, f32[1,3,2,1,32,256]{5,4,3,2,1,0:T(8,128)S(1)}, u32[]{:S(2)}, u32[]{:S(2)}) collective-permute-start(f32[1,3,2,1,32,256]{5,4,3,2,1,0:T(8,128)S(1)} %slice.2254), channel_id=1, source_target_pairs={{2,0},{4,2},{6,4},{8,6},{10,8},{12,10},{14,12},{3,1},{5,3},{7,5},{... | collective-permute-start | bytes 589832 | tf_op jit(solution)/shard_map/ppermute | solution.py:15
  345.1 3.1 collective-permute-start.17
  353.5 5.3 %collective-permute-start.19 = (f32[1,3,2,1,32,256]{5,4,3,2,1,0:T(8,128)S(1)}, f32[1,3,2,1,32,256]{5,4,3,2,1,0:T(8,128)S(1)}, u32[]{:S(2)}, u32[]{:S(2)}) collective-permute-start(f32[1,3,2,1,32,256]{5,4,3,2,1,0:T(8,128)S(1)} %pad_maximum_fusion.25), channel_id=1, source_target_pairs={{0,2},{2,4},{4,6},{6,8},{8,10},{10,12},{12,14},{1,3},{3,5},{5,7},{... | collective-permute-start | bytes 589832 | tf_op jit(solution)/shard_map/ppermute | solution.py:15
  355.0 2.1 collective-permute-start.18
  410.7 23.8 %copy-start.38 = (f32[1,3,1,4,32,256]{5,4,3,2,1,0:T(8,128)}, f32[1,3,1,4,32,256]{5,4,3,2,1,0:T(8,128)S(1)}, u32[]{:S(2)}) copy-start(f32[1,3,1,4,32,256]{5,4,3,2,1,0:T(8,128)S(1)} %get-tuple-element.84) | copy-start | bytes 1179652
  410.7 23.8 %copy-start.40 = (f32[1,3,1,4,32,256]{5,4,3,2,1,0:T(8,128)}, f32[1,3,1,4,32,256]{5,4,3,2,1,0:T(8,128)S(1)}, u32[]{:S(2)}) copy-start(f32[1,3,1,4,32,256]{5,4,3,2,1,0:T(8,128)S(1)} %get-tuple-element.85) | copy-start | bytes 1179652
  410.7 4.9 %copy-start.6 = (f32[1,3,2,4,32,256]{5,4,3,2,1,0:T(8,128)S(1)}, f32[1,3,2,4,32,256]{5,4,3,2,1,0:T(8,128)}, u32[]{:S(2)}) copy-start(f32[1,3,2,4,32,256]{5,4,3,2,1,0:T(8,128)} %copy-done.5) | copy-start | bytes 2359300
  413.1 4.9 %collective-permute-start.21 = (f32[1,3,2,4,1,256]{5,4,3,2,1,0:T(1,128)S(1)}, f32[1,3,2,4,1,256]{5,4,3,2,1,0:T(1,128)S(1)}, u32[]{:S(2)}, u32[]{:S(2)}) collective-permute-start(f32[1,3,2,4,1,256]{5,4,3,2,1,0:T(1,128)S(1)} %slice.2299), channel_id=1, source_target_pairs={{1,0},{3,2},{5,4},{7,6},{9,8},{11,10},{13,12},{15,14},{17,16},{19,... | collective-permute-start | bytes 73736 | tf_op jit(solution)/shard_map/ppermute | solution.py:15
  414.4 9.5 %collective-permute-start.20 = (f32[1,3,2,1,32,256]{5,4,3,2,1,0:T(8,128)S(1)}, f32[1,3,2,1,32,256]{5,4,3,2,1,0:T(8,128)S(1)}, u32[]{:S(2)}, u32[]{:S(2)}) collective-permute-start(f32[1,3,2,1,32,256]{5,4,3,2,1,0:T(8,128)S(1)} %slice.2295), channel_id=1, source_target_pairs={{2,0},{4,2},{6,4},{8,6},{10,8},{12,10},{14,12},{3,1},{5,3},{7,5},{... | collective-permute-start | bytes 589832 | tf_op jit(solution)/shard_map/ppermute | solution.py:15
  425.6 6.1 %collective-permute-start.22 = (f32[1,3,2,4,1,256]{5,4,3,2,1,0:T(1,128)S(1)}, f32[1,3,2,4,1,256]{5,4,3,2,1,0:T(1,128)S(1)}, u32[]{:S(2)}, u32[]{:S(2)}) collective-permute-start(f32[1,3,2,4,1,256]{5,4,3,2,1,0:T(1,128)S(1)} %pad_maximum_fusion.35), channel_id=1, source_target_pairs={{0,1},{2,3},{4,5},{6,7},{8,9},{10,11},{12,13},{14,15},{16,17},{18,... | collective-permute-start | bytes 73736 | tf_op jit(solution)/shard_map/ppermute | solution.py:15
  427.6 5.3 %collective-permute-start.23 = (f32[1,3,2,1,32,256]{5,4,3,2,1,0:T(8,128)S(1)}, f32[1,3,2,1,32,256]{5,4,3,2,1,0:T(8,128)S(1)}, u32[]{:S(2)}, u32[]{:S(2)}) collective-permute-start(f32[1,3,2,1,32,256]{5,4,3,2,1,0:T(8,128)S(1)} %pad_maximum_fusion.23), channel_id=1, source_target_pairs={{0,2},{2,4},{4,6},{6,8},{8,10},{10,12},{12,14},{1,3},{3,5},{5,7},{... | collective-permute-start | bytes 589832 | tf_op jit(solution)/shard_map/ppermute | solution.py:15
  437.5 3.6 copy-start.8
  481.8 4.0 copy-start.15
  481.8 4.0 copy-start.22
  481.8 4.0 copy-start.25
  481.8 4.0 copy-start.39
  481.8 4.0 copy-start.41
  485.9 2.1 copy-start.49
  485.9 2.2 copy-start.50
  485.9 2.3 copy-start.51
  (46 other events, 43.7 us)
